TPU v7x, 32 devices: a whole 2x2x4 slice. The times are simulated.
32 devices in a mesh: groups: 2 (over y), seq: 4 (over z), head: 4 (over x, core).
Axes of the slice: x: 2, y: 2, z: 4, core: 2. Of those that a mesh axis runs over, the one named last changes fastest.
Arguments:
- residual: bfloat16 [4096, 2560], P(('groups', 'seq'), 'head'), parts along dimension 0, may hold values from -6 to 6
- x_in: bfloat16 [4096, 5120], P(('groups', 'seq'), 'head'), parts along dimension 0, may hold values from -6 to 6
- bc_in: bfloat16 [4096, 256], P(('groups', 'seq')), parts along dimension 0, may hold values from -1.5 to 1.5
- z_in: bfloat16 [4096, 5120], P(('groups', 'seq'), 'head'), parts along dimension 0, may hold values from -6 to 6
- dt_raw: float32 [80, 4096], P('head', ('groups', 'seq')), parts along dimension 1, may hold values from -5 to 5
- dt_bias: float32 [80], P('head'), may hold values from -3 to 0
- decay_rate: float32 [80], P('head'), may hold values from 0.0003 to 0.15
- d_skip: float32 [80], P('head'), may hold values from 1 to 4
- conv_x_weight: bfloat16 [4, 5120], P(None, 'head'), may hold values from -3 to 3
- conv_x_bias: bfloat16 [5120], P('head'), may hold values from -3 to 3
- conv_bc_weight: bfloat16 [4, 256], replicated, may hold values from -3 to 3
- conv_bc_bias: bfloat16 [256], replicated, may hold values from -3 to 3
- norm_gain: bfloat16 [5120], P('head'), may hold values from 0.5 to 1.5
- out_weight: bfloat16 [5120, 2560], P('head'), may hold values from -0.078125 to 0.078125
- final_gain: bfloat16 [2560], replicated, may hold values from 0.5 to 1.5
- lm_weight: bfloat16 [2560, 25600], P('seq', 'head'), may hold values from -15.811388 to 15.811388
- targets: int32 [4096], P(('groups', 'seq')), parts along dimension 0, may hold values from 0 to 25599
- doc_lengths: int32 [8], P('groups'), parts along dimension 0, may hold values from 1 to 1536, as said below
Outputs:
- block_out: bfloat16 [4096, 2560], P(('groups', 'seq'), 'head'), parts along dimension 0
- doc_loss: float32 [8], P('groups'), parts along dimension 0
There are 2 independent parts, one for each index of `groups`. A program takes and returns all parts, laid end to end along the dimension named above; an argument that names none is the same for every part. Nothing has to cross between parts.
Inputs may be any that keep to these rules, and one draw needn't show every extreme that they name: `doc_lengths`: the lengths of a group's 4 documents, in the order in which they are packed into its 2048 tokens; they sum to 2048.
All inputs are finite; a program needn't handle non-finite values.
Results may differ from a plain program's by a relative error of at most 0.00145.
The roundings to bfloat16 on the way count: a program that leaves them out, or rounds other values in their place, can miss the bound.
Values may be sent and summed in bfloat16 or wider, within the bound.
A program may use at most 128 MiB of HBM per device.

v0:
```python
import functools

import jax
import jax.numpy as jnp
from jax import lax
from jax.experimental import pallas as pl
from jax.experimental.pallas import tpu as pltpu
from jax.sharding import PartitionSpec as P

D = 2560
HEAD_SIZE = 64
STATE = 128
KERNEL = 4
SPAN = 256
INNER = 5120


EPSILON = 1e-05
HIGH = lax.Precision.HIGHEST
HALF = lax.Precision.HIGH
LOW = -1e30
MESH = pl.DeviceIdType.MESH


def shifted(array, axis, by):
    length = lax.axis_size(axis)
    pairs = [(i, i + by) for i in range(length) if 0 <= i + by < length]
    return lax.ppermute(array, axis, pairs)


def rotated(array, axis, by):
    length = lax.axis_size(axis)
    return lax.ppermute(array, axis, [(i, (i + by) % length) for i in range(length)])


def sibling(array, axis):
    length = lax.axis_size(axis)
    return lax.ppermute(array, axis, [(i, i ^ 1) for i in range(length)])


def scattered_product(normed, weight, axis):
    length = lax.axis_size(axis)
    rank = lax.axis_index(axis)
    chips = length // 2
    share = weight.shape[1] // length

    def columns(core):
        return jnp.concatenate(
            [
                lax.dynamic_slice_in_dim(
                    weight, ((rank // 2 + by) % chips * 2 + core) * share, share, 1
                )
                for by in range(chips)
            ],
            axis=1,
        )

    theirs = columns(1 - rank % 2)
    ours = columns(rank % 2)
    other = jnp.dot(normed, theirs, preferred_element_type=jnp.float32)
    arrived = sibling(other, axis)
    pair = jnp.dot(normed, ours, preferred_element_type=jnp.float32) + arrived
    total = pair[:, :share]
    for by in range(1, chips):
        total = total + rotated(pair[:, by * share : (by + 1) * share], axis, 2 * by)
    return total


def gathered_features(part, axis):
    length = lax.axis_size(axis)
    rank = lax.axis_index(axis)
    chips = length // 2
    rows, share = part.shape
    column = [part] + [rotated(part, axis, 2 * by) for by in range(1, chips)]
    joined = jnp.concatenate(column, axis=1)
    twin = sibling(joined, axis)
    full = jnp.zeros((rows, share * length), part.dtype)
    for by in range(chips):
        source = (rank + 2 * (chips - by)) % length
        piece = slice(by * share, (by + 1) * share)
        full = lax.dynamic_update_slice_in_dim(full, joined[:, piece], source * share, 1)
        full = lax.dynamic_update_slice_in_dim(full, twin[:, piece], (source ^ 1) * share, 1)
    return full


def entering(through, state, axis):
    length = lax.axis_size(axis)
    tag = jnp.broadcast_to(through[:, None, None], (through.shape[0], 8, state.shape[2]))
    packed = shifted(jnp.concatenate([state, tag], axis=1), axis, 1)
    extent = state.shape[1]
    reach = 1
    while reach < length:
        earlier = shifted(packed, axis, reach)
        decay = packed[:, extent : extent + 1, :]
        packed = jnp.concatenate(
            [packed[:, :extent] + decay * earlier[:, :extent], decay * earlier[:, extent:]], axis=1
        )
        reach *= 2
    return packed[:, :extent]


def document_of(positions, doc_lengths):
    starts = jnp.cumsum(doc_lengths) - doc_lengths
    return jnp.sum((positions[:, None] >= starts[None, :]).astype(jnp.int32), axis=1) - 1


def causal_conv(signal, rim_rows, weight, bias, positions, doc_ids, doc_lengths):
    length = signal.shape[0]
    taps = weight.shape[0]
    joined = jnp.concatenate([rim_rows, signal], axis=0).astype(jnp.float32)
    total = jnp.zeros(signal.shape, jnp.float32) + bias.astype(jnp.float32)[None, :]
    for offset in range(taps):
        lag = taps - 1 - offset
        source = document_of(positions - lag, doc_lengths)
        same = (source == doc_ids).astype(jnp.float32)
        total = (
            total
            + weight[offset].astype(jnp.float32)[None, :]
            * joined[offset : offset + length]
            * same[:, None]
        )
    return jax.nn.silu(total).astype(jnp.bfloat16)


def conv_state_kernel(x_ref, rim_ref, taps_ref, bias_ref, same_ref, cols_ref, bmat_ref, values_ref, state_ref, held):
    length, lanes = x_ref.shape
    taps = taps_ref.shape[0]
    held[0:8, :] = rim_ref[...].astype(jnp.float32)
    held[8:, :] = x_ref[...].astype(jnp.float32)
    total = jnp.zeros((length, lanes), jnp.float32) + bias_ref[...]
    for offset in range(taps):
        lag = taps - 1 - offset
        rows = held[8 - lag : 8 - lag + length, :]
        total = total + taps_ref[offset : offset + 1, :] * rows * same_ref[:, lag : lag + 1]
    values = jax.nn.silu(total).astype(jnp.bfloat16)
    values_ref[...] = values
    first = lax.broadcasted_iota(jnp.int32, (length, lanes), 1) < HEAD_SIZE
    tail = jnp.where(first, cols_ref[0, :, 2:3], cols_ref[0, :, 3:4])
    scaled = values.astype(jnp.float32) * tail
    high = scaled.astype(jnp.bfloat16)
    low = (scaled - high.astype(jnp.float32)).astype(jnp.bfloat16)
    bmat = bmat_ref[...]
    dims = (((0,), (0,)), ((), ()))
    state_ref[...] = lax.dot_general(
        high, bmat, dims, preferred_element_type=jnp.float32
    ) + lax.dot_general(low, bmat, dims, preferred_element_type=jnp.float32)


def within_kernel(values_ref, scores_ref, cols_ref, rows_ref, skip_ref, out_ref):
    length, lanes = values_ref.shape
    for cut in range(0, length, SPAN):
        upto = cut + SPAN
        values = values_ref[0:upto, :]
        scores = scores_ref[cut:upto, 0:upto]
        parts = []
        for which in range(2):
            gap = rows_ref[0, which : which + 1, 0:upto] - cols_ref[0, cut:upto, which : which + 1]
            weights = (
                jnp.exp(jnp.minimum(gap, 0.0)) * scores * rows_ref[0, 2 + which : 3 + which, 0:upto]
            )
            high = weights.astype(jnp.bfloat16)
            low = (weights - high.astype(jnp.float32)).astype(jnp.bfloat16)
            parts.append(
                jnp.dot(high, values, preferred_element_type=jnp.float32)
                + jnp.dot(low, values, preferred_element_type=jnp.float32)
            )
        first = lax.broadcasted_iota(jnp.int32, (SPAN, lanes), 1) < HEAD_SIZE
        own = values_ref[cut:upto, :].astype(jnp.float32)
        out_ref[cut:upto, :] = jnp.where(first, parts[0], parts[1]) + skip_ref[...] * own


def conv_state(x_in, rim, taps, bias, same, cols, bmat):
    length, inner_here = x_in.shape
    lanes = 2 * HEAD_SIZE
    return pl.pallas_call(
        conv_state_kernel,
        grid=(inner_here // lanes,),
        in_specs=[
            pl.BlockSpec((length, lanes), lambda i: (0, i)),
            pl.BlockSpec((8, lanes), lambda i: (0, i)),
            pl.BlockSpec((taps.shape[0], lanes), lambda i: (0, i)),
            pl.BlockSpec((1, lanes), lambda i: (0, i)),
            pl.BlockSpec(same.shape, lambda i: (0, 0)),
            pl.BlockSpec((1, length, 4), lambda i: (i, 0, 0)),
            pl.BlockSpec(bmat.shape, lambda i: (0, 0)),
        ],
        out_specs=[
            pl.BlockSpec((length, lanes), lambda i: (0, i)),
            pl.BlockSpec((lanes, STATE), lambda i: (i, 0)),
        ],
        out_shape=[
            jax.ShapeDtypeStruct((length, inner_here), jnp.bfloat16),
            jax.ShapeDtypeStruct((inner_here, STATE), jnp.float32),
        ],
        scratch_shapes=[pltpu.VMEM((length + 8, lanes), jnp.float32)],
        cost_estimate=pl.CostEstimate(flops=10**9, bytes_accessed=6 * 10**6, transcendentals=10**6),
    )(x_in, rim, taps, bias, same, cols, bmat)


def within(values, scores, cols, rows, skip):
    length, inner_here = values.shape
    lanes = 2 * HEAD_SIZE
    return pl.pallas_call(
        within_kernel,
        grid=(inner_here // lanes,),
        in_specs=[
            pl.BlockSpec((length, lanes), lambda i: (0, i)),
            pl.BlockSpec(scores.shape, lambda i: (0, 0)),
            pl.BlockSpec((1, length, 4), lambda i: (i, 0, 0)),
            pl.BlockSpec((1, 4, length), lambda i: (i, 0, 0)),
            pl.BlockSpec((1, lanes), lambda i: (0, i)),
        ],
        out_specs=pl.BlockSpec((length, lanes), lambda i: (0, i)),
        out_shape=jax.ShapeDtypeStruct((length, inner_here), jnp.float32),
        cost_estimate=pl.CostEstimate(flops=8 * 10**9, bytes_accessed=20 * 10**6, transcendentals=10**7),
    )(values, scores, cols, rows, skip)


TILE = 128
LOSS_ROWS = 256
HALO = 16
PARTS = 4


def block_kernel(
    n, heads, groups, inner, features, widths,
    x_ref, z_ref, bc_ref, taps_ref, bc_taps_ref, res_ref, tgt_ref, dt_ref, table_ref,
    lens_ref, dt_bias_ref, rate_ref, skip_ref, ow_ref, lm_ref,
    block_ref, out_ref,
    ow_buf, w_buf, full, tgts, marks, parts, sums, halo_x, halo_bc, held, masks, carried, rows, cols, values, keys,
    scores, state_out, state_in, gated, squares, tiles, normed, share_out, share_in, hid,
    load_sem, halo_send, halo_recv, w_send, w_recv, y_send, y_recv, state_send, state_recv,
    tile_send, tile_recv, share_send, share_recv,
    along_send, side_send, arrive, tgt_send, tgt_recv, mark_send, mark_recv, sum_send, sum_recv,
):
    g = lax.axis_index("groups")
    z = lax.axis_index("seq")
    h = lax.axis_index("head")
    length, inner_here = x_ref.shape
    share = res_ref.shape[1]
    depth, columns = lm_ref.shape
    starts = [sum(widths[:rank]) for rank in range(n)]
    band = depth // groups
    sub = band // PARTS
    total_peers = n * heads
    me = z * heads + h
    twin = h + 1 - 2 * lax.rem(h, 2)
    side = lax.rem(h + 2, heads)
    chunks = inner_here // TILE

    def remote(src, dst, send, recv, target):
        return pltpu.make_async_remote_copy(
            src_ref=src, dst_ref=dst, send_sem=send, recv_sem=recv,
            device_id=target, device_id_type=MESH,
        )

    def peer(k):
        flat = lax.rem(me + k, total_peers)
        return flat // heads, lax.rem(flat, heads)

    load_out = pltpu.make_async_copy(ow_ref, ow_buf, load_sem.at[0])
    load_out.start()

    def load_own(rank):
        return pltpu.make_async_copy(
            lm_ref.at[:, pl.ds(starts[rank], widths[rank])],
            w_buf.at[pl.ds(rank * depth, depth), pl.ds(0, widths[rank])],
            load_sem.at[1],
        )

    for rank in range(n):
        @pl.when(z == rank)
        def _():
            load_own(rank).start()

    barrier = pltpu.get_barrier_semaphore()

    @pl.loop(1, total_peers)
    def _(k):
        there, where_head = peer(k)
        pl.semaphore_signal(
            barrier, inc=1, device_id={"seq": there, "head": where_head}, device_id_type=MESH
        )

    for hop in range(1, groups):
        pl.semaphore_signal(
            barrier, inc=1, device_id={"groups": lax.rem(g + hop, groups)}, device_id_type=MESH
        )
    pl.semaphore_wait(barrier, total_peers - 1 + groups - 1)

    def halo_copies():
        tail_rows = pl.ds(length - HALO, HALO)
        return [
            remote(x_ref.at[tail_rows, :], halo_x, halo_send.at[0], halo_recv.at[0], {"seq": z + 1}),
            remote(bc_ref.at[tail_rows, :], halo_bc, halo_send.at[1], halo_recv.at[1], {"seq": z + 1}),
        ]

    @pl.when(z < n - 1)
    def _():
        for copy in halo_copies():
            copy.start()

    def w_rows(source, group, part):
        return pl.ds(pl.multiple_of(source * depth + group * band + part * sub, 16), sub)

    def w_copy(rank, part):
        columns_there = pl.ds(starts[rank], widths[rank])
        return remote(
            lm_ref.at[pl.ds(pl.multiple_of(g * band + part * sub, 16), sub), columns_there],
            w_buf.at[w_rows(z, g, part), pl.ds(0, widths[rank])],
            w_send.at[rank, part],
            w_recv.at[z, part],
            {"seq": rank},
        )

    def w_place(rank, source, group, part):
        return w_buf.at[w_rows(source, group, part), pl.ds(0, widths[rank])]

    def w_forward(rank, source, part, hop):
        place = w_place(rank, source, g, part)
        return remote(
            place, place, y_send.at[source, part, hop], y_recv.at[g, source, part],
            {"groups": lax.rem(g + hop, groups)},
        )

    def w_pass_on(rank, source, part):
        place = w_place(rank, source, g, part)
        remote(
            place, place, w_send.at[source, part], w_recv.at[source, part], {"seq": source}
        ).wait_recv()
        for hop in range(1, groups):
            w_forward(rank, source, part, hop).start()

    def legs(rank):
        far_first = list(range(n - 1, rank, -1)) + list(range(rank))
        every = [(source, part) for source in far_first for part in range(PARTS)]

        def early(source, part):
            if source < rank:
                return source == rank - 1 and (part == 0 or rank in (1, n - 1))
            if rank == 0:
                return source != 2
            return source > rank + 1 or (rank == n - 2 and part < PARTS // 2)

        return [leg for leg in every if early(*leg)], [leg for leg in every if not early(*leg)]

    for rank in range(n):
        @pl.when(z > rank)
        def _():
            for part in range(PARTS):
                w_copy(rank, part).start()

        @pl.when(z + 1 == rank)
        def _():
            w_copy(rank, 0).start()

    def tell(k, source):
        return remote(
            tgt_ref, tgts.at[source], tgt_send.at[k], tgt_recv.at[source],
            {"seq": lax.rem(z + k, n)},
        )

    for k in range(1, n):
        tell(k, z).start()
    tgts[z] = tgt_ref[...]

    starts_of = [jnp.int32(0)]
    for document in range(lens_ref.shape[0] - 1):
        starts_of.append(starts_of[-1] + lens_ref[document])

    def document(positions):
        total = (positions >= starts_of[0]).astype(jnp.int32)
        for start in starts_of[1:]:
            total = total + (positions >= start).astype(jnp.int32)
        return total

    offset_here = z * length

    def along(shape, axis):
        return lax.broadcasted_iota(jnp.int32, shape, axis) + offset_here

    here_heads = dt_ref.shape[0]
    head_row = lax.broadcasted_iota(jnp.int32, (here_heads, length), 0)
    lane_row = lax.broadcasted_iota(jnp.int32, (here_heads, length), 1)
    shift = jnp.zeros((here_heads, length), jnp.float32)
    rate = jnp.zeros((here_heads, length), jnp.float32)
    for head in range(here_heads):
        shift = jnp.where(head_row == head, dt_bias_ref[head], shift)
        rate = jnp.where(head_row == head, rate_ref[head], rate)
    raw = dt_ref[...] + shift
    steps = jnp.maximum(raw, 0.0) + jnp.log1p(jnp.exp(-jnp.abs(raw)))
    climb = steps * rate
    by = 1
    while by < length:
        climb = climb + jnp.where(lane_row >= by, pltpu.roll(climb, by, 1), 0.0)
        by *= 2
    is_last = document(along((here_heads, length), 1)) == document(offset_here + length - 1)
    leave = jnp.where(is_last, jnp.exp(climb - climb[:, length - 1 :]) * steps, 0.0)
    for c in range(chunks):
        pair = slice(2 * c, 2 * c + 2)
        rows[c, 0:2, :] = climb[pair]
        rows[c, 2:4, :] = steps[pair]
        rows[c, 4:6, :] = leave[pair]
        rows[c, 6:8, :] = leave[pair]

    token = along((length, TILE), 0)
    at_token = document(token)
    for lag in range(1, KERNEL):
        masks[lag - 1] = (document(token - lag) == at_token).astype(jnp.float32)
    carried[...] = (at_token == document(offset_here - 1)).astype(jnp.float32)

    @pl.when(z == 0)
    def _():
        halo_x[...] = jnp.zeros_like(halo_x)
        halo_bc[...] = jnp.zeros_like(halo_bc)
        state_in[...] = jnp.zeros_like(state_in)

    @pl.when(z > 0)
    def _():
        for copy in halo_copies():
            copy.wait_recv()

    def convolved(signal, halo, weight, bias, lanes):
        weight = weight[:, lanes].astype(jnp.float32)
        held[0:HALO, :] = halo[:, lanes].astype(jnp.float32)
        held[HALO:, :] = signal[:, lanes].astype(jnp.float32)
        total = jnp.zeros((length, TILE), jnp.float32) + bias
        for offset in range(KERNEL):
            lag = KERNEL - 1 - offset
            term = weight[offset : offset + 1, :] * held[HALO - lag : HALO - lag + length, :]
            total = total + (term * masks[lag - 1] if lag else term)
        return jax.nn.silu(total).astype(jnp.bfloat16)

    def line(at):
        return table_ref[pl.ds(at, 1), :]

    for half in range(2):
        lanes = pl.ds(half * STATE, STATE)
        keys[:, lanes] = convolved(bc_ref, halo_bc, bc_taps_ref, line(2 * chunks + half), lanes)
    nt = (((1,), (1,)), ((), ()))
    for cut in range(0, length, SPAN):
        near = pl.ds(cut, SPAN)
        target, source = along((SPAN, length), 0) + cut, along((SPAN, length), 1)
        inside = (document(target) == document(source)) & (target >= source)
        product = lax.dot_general(
            keys[near, STATE:], keys[:, :STATE], nt, preferred_element_type=jnp.float32
        )
        scores[near, :] = jnp.where(inside, product, 0.0)

    def state_copy(c):
        return remote(
            state_out.at[c], state_in.at[c], state_send.at[c], state_recv.at[c], {"seq": z + 1}
        )

    first = lax.broadcasted_iota(jnp.int32, (SPAN, TILE), 1) < HEAD_SIZE

    @pl.loop(0, chunks)
    def _(c):
        lanes = pl.ds(pl.multiple_of(c * TILE, TILE), TILE)
        own = convolved(x_ref, halo_x, taps_ref, line(c), lanes)
        values[:, lanes] = own
        early = lax.broadcasted_iota(jnp.int32, (length, TILE), 1) < HEAD_SIZE
        cols[c] = jnp.transpose(rows[c])
        decay = jnp.where(early, cols[c, :, 4:5], cols[c, :, 5:6])
        scaled = own.astype(jnp.float32) * decay
        high = scaled.astype(jnp.bfloat16)
        low = (scaled - high.astype(jnp.float32)).astype(jnp.bfloat16)
        bmat = keys[:, :STATE]
        tn = (((0,), (0,)), ((), ()))
        state_out[c] = lax.dot_general(
            high, bmat, tn, preferred_element_type=jnp.float32
        ) + lax.dot_general(low, bmat, tn, preferred_element_type=jnp.float32)

        @pl.when(z == 0)
        def _():
            state_copy(c).start()

    squares[...] = jnp.zeros_like(squares)

    @pl.loop(0, chunks)
    def _(c):
        lanes = pl.ds(pl.multiple_of(c * TILE, TILE), TILE)

        @pl.when(z > 0)
        def _():
            state_copy(c).wait_recv()

        @pl.when((z > 0) & (z < n - 1))
        def _():
            top = lax.broadcasted_iota(jnp.int32, (TILE, STATE), 0) < HEAD_SIZE
            final = cols[c, length - 1 : length, 0:2]
            through = jnp.where(top, jnp.exp(-final[:, 0:1]), jnp.exp(-final[:, 1:2]))
            through = through * carried[length - 1 : length, 0:1]
            state_out[c] = through * state_in[c] + state_out[c]
            state_copy(c).start()

        skip = jnp.where(first, skip_ref[2 * c], skip_ref[2 * c + 1])
        incoming = state_in[c]
        in_high = incoming.astype(jnp.bfloat16)
        in_low = (incoming - in_high.astype(jnp.float32)).astype(jnp.bfloat16)
        for cut in range(0, length, SPAN):
            upto = cut + SPAN
            near = pl.ds(cut, SPAN)
            signal = values[0:upto, lanes]
            sums_of = []
            entries = []
            for which in range(2):
                climb = cols[c, near, which : which + 1]
                gap = rows[c, which : which + 1, 0:upto] - climb
                weights = (
                    jnp.exp(jnp.minimum(gap, 0.0))
                    * scores[near, 0:upto]
                    * rows[c, 2 + which : 3 + which, 0:upto]
                )
                high = weights.astype(jnp.bfloat16)
                low = (weights - high.astype(jnp.float32)).astype(jnp.bfloat16)
                sums_of.append(
                    jnp.dot(high, signal, preferred_element_type=jnp.float32)
                    + jnp.dot(low, signal, preferred_element_type=jnp.float32)
                )
                entries.append(jnp.exp(-climb))
            cmat = keys[near, STATE:]
            arriving = lax.dot_general(
                cmat, in_high, nt, preferred_element_type=jnp.float32
            ) + lax.dot_general(cmat, in_low, nt, preferred_element_type=jnp.float32)
            mixed = (
                jnp.where(first, sums_of[0], sums_of[1])
                + skip * values[near, lanes].astype(jnp.float32)
                + arriving * (jnp.where(first, entries[0], entries[1]) * carried[near, :])
            )
            result = mixed * jax.nn.silu(z_ref[near, lanes].astype(jnp.float32))
            gated[near, lanes] = result
            squares[near, :] += result * result

    for rank in range(1, n):
        @pl.when(z + 1 == rank)
        def _():
            for part in range(1, PARTS):
                w_copy(rank, part).start()

        @pl.when(z + 1 < rank)
        def _():
            for part in range(PARTS):
                w_copy(rank, part).start()

    def tile_copy(which, k, slot_of):
        return remote(
            tiles.at[which, slot_of], tiles.at[which, slot_of], tile_send.at[which, k],
            tile_recv.at[which, slot_of], {"head": lax.rem(h + k, heads)},
        )

    def scale_of(which, partial, count):
        column = jnp.broadcast_to(jnp.sum(partial, axis=1, keepdims=True), (length, TILE))
        tiles[which, h] = jnp.transpose(column)[0:8, :]
        for k in range(1, heads):
            tile_copy(which, k, h).start()
        for k in range(1, heads):
            tile_copy(which, k, lax.rem(h + k, heads)).wait()
        total = tiles[which, 0]
        for head in range(1, heads):
            total = total + tiles[which, head]
        scale = lax.rsqrt(total / count + EPSILON)
        return jnp.transpose(jnp.broadcast_to(scale[0:1, :], (TILE, length)))

    squares[...] = scale_of(0, squares[...], inner)

    @pl.loop(0, chunks)
    def _(c):
        lanes = pl.ds(pl.multiple_of(c * TILE, TILE), TILE)
        normed[:, lanes] = (gated[:, lanes] * squares[...] * line(chunks + c)).astype(jnp.bfloat16)

    load_out.wait()

    def project(head, slot_of):
        @pl.loop(0, length // LOSS_ROWS)
        def _(step):
            near = pl.ds(pl.multiple_of(step * LOSS_ROWS, LOSS_ROWS), LOSS_ROWS)
            share_out[slot_of, near, :] = jnp.dot(
                normed[near, :],
                ow_buf[:, pl.ds(pl.multiple_of(head * share, TILE), share)],
                preferred_element_type=jnp.float32,
            )

    def share_copy(slot_of, target):
        return remote(
            share_out.at[slot_of], share_in.at[slot_of], share_send.at[slot_of],
            share_recv.at[slot_of], {"head": target},
        )

    project(lax.rem(twin + 2, heads), 0)
    share_copy(0, twin).start()
    project(side, 1)
    share_copy(0, twin).wait_recv()
    share_out[1] = share_out[1] + share_in[0]
    share_copy(1, side).start()
    project(twin, 2)
    share_copy(2, twin).start()
    project(h, 3)

    for rank in range(n):
        @pl.when(z == rank)
        def _():
            for source, part in legs(rank)[0]:
                w_pass_on(rank, source, part)

    share_copy(2, twin).wait_recv()
    share_copy(1, side).wait_recv()

    @pl.loop(0, length // LOSS_ROWS)
    def _(step):
        near = pl.ds(pl.multiple_of(step * LOSS_ROWS, LOSS_ROWS), LOSS_ROWS)
        total = share_out[3, near, :] + share_in[2, near, :] + share_in[1, near, :]
        block_ref[near, :] = (res_ref[near, :].astype(jnp.float32) + total).astype(jnp.bfloat16)

    square = jnp.zeros((length, TILE), jnp.float32)
    for cut in range(0, share, TILE):
        piece = block_ref[:, cut : cut + TILE].astype(jnp.float32)
        square = square + piece * piece
    squares[...] = scale_of(1, square, features)
    for cut in range(0, share, TILE):
        piece = block_ref[:, cut : cut + TILE].astype(jnp.float32)
        hid[:, cut : cut + TILE] = (
            piece * squares[...] * line(2 * chunks + 2 + h * (share // TILE) + cut // TILE)
        ).astype(jnp.bfloat16)

    full[z, :, pl.ds(pl.multiple_of(h * share, TILE), share)] = hid[...]

    half_rows = length // 2

    def near_of(half):
        start = half * half_rows
        return pl.ds(start if isinstance(start, int) else pl.multiple_of(start, 16), half_rows)

    def slot(block, head, half):
        near = near_of(half)
        return full.at[block, near, pl.ds(pl.multiple_of(head * share, TILE), share)]

    def ship(sems, block, head, half, target, first=False):
        place = slot(block, head, half)
        return remote(
            hid.at[near_of(half), :] if first else place, place,
            sems.at[block, half], arrive.at[block, head, half], target,
        )

    def right(block, half, first=False):
        return ship(along_send.at[0], block, h, half, {"seq": z + 1}, first)

    def left(block, half, first=False):
        return ship(along_send.at[1], block, h, half, {"seq": z - 1}, first)

    def across(block, half, first=False):
        return ship(side_send, block, h, half, {"head": side}, first)

    def twinned(kind, block, head, half, first=False):
        return ship(along_send.at[2 + kind], block, head, half, {"head": twin}, first)

    def arrived(block, head, half):
        twinned(0, block, head, half).wait_recv()

    for half in range(2):
        @pl.when(z < n - 1)
        def _():
            right(z, half, True).start()

        @pl.when(z > 0)
        def _():
            left(z, half, True).start()

        across(z, half, True).start()
        twinned(0, z, h, half, True).start()

    def mark_copy(block, head):
        return remote(
            marks.at[block, :, pl.ds(pl.multiple_of(head * TILE, TILE), TILE)], parts.at[me],
            mark_send.at[block, head], mark_recv.at[me], {"seq": block, "head": head},
        )

    live, start_column = widths[0], 0
    for rank in range(1, n):
        live = jnp.where(z == rank, widths[rank], live)
        start_column = jnp.where(z == rank, starts[rank], start_column)
    start_column = h * columns + start_column
    width = w_buf.shape[1]

    def compute(block, half):
        @pl.loop(0, half_rows // LOSS_ROWS)
        def _(step):
            at = pl.multiple_of(half * half_rows + step * LOSS_ROWS, LOSS_ROWS)
            logits = jnp.dot(
                full[block, pl.ds(at, LOSS_ROWS), :], w_buf[...], preferred_element_type=jnp.float32
            )
            wanted = []
            for cut in range(LOSS_ROWS // TILE):
                row = tgts[block, pl.ds(lax.div(at, TILE) + cut, 1), :]
                wanted.append(jnp.transpose(jnp.broadcast_to(row, (TILE, TILE))))
            wanted = jnp.concatenate(wanted, axis=0) - start_column
            lane = lax.broadcasted_iota(jnp.int32, (LOSS_ROWS, TILE), 1)
            pieces = []
            for cut in range(0, width, TILE):
                piece = logits[:, cut : cut + TILE]
                if cut + TILE > min(widths):
                    piece = jnp.where(lane + cut < live, piece, LOW)
                pieces.append(piece)
            peak = pieces[0]
            for piece in pieces[1:]:
                peak = jnp.maximum(peak, piece)
            peak = jnp.max(peak, axis=1, keepdims=True)
            total = jnp.zeros((LOSS_ROWS, TILE), jnp.float32)
            picked = jnp.zeros((LOSS_ROWS, TILE), jnp.float32)
            for index, piece in enumerate(pieces):
                total = total + jnp.exp(piece - peak)
                here = lane + index * TILE == wanted
                if (index + 1) * TILE > min(widths):
                    here = here & (lane + index * TILE < live)
                picked = picked + jnp.where(here, piece, 0.0)
            total = jnp.sum(total, axis=1, keepdims=True)
            picked = jnp.sum(picked, axis=1, keepdims=True)
            tile = jnp.where(lane == 0, peak, jnp.where(lane == 1, total, picked))
            marks[block, :, pl.ds(at, LOSS_ROWS)] = jnp.transpose(tile)[0:8, :]

        @pl.loop(half * (heads // 2), (half + 1) * (heads // 2))
        def _(head):
            @pl.when((block != z) | (head != h))
            def _():
                mark_copy(block, head).start()

    def relay(block, half):
        arrived(block, side, half)
        twinned(1, block, side, half).start()

    def finish(block, half):
        arrived(block, twin, half)
        arrived(block, lax.rem(twin + 2, heads), half)
        compute(block, half)

    for rank in range(n):
        @pl.when(z == rank)
        def _():
            for source, part in legs(rank)[1]:
                w_pass_on(rank, source, part)

    def embedding_here():
        for k in range(1, n):
            tell(k, lax.rem(z + n - k, n)).wait()
        for rank in range(n):
            @pl.when(z == rank)
            def _():
                load_own(rank).wait()
                for source in range(n):
                    if source == rank:
                        continue
                    for hop in range(1, groups):
                        other = lax.rem(g + groups - hop, groups)
                        for part in range(PARTS):
                            place = w_place(rank, source, other, part)
                            remote(
                                place, place, y_send.at[source, part, hop],
                                y_recv.at[other, source, part], {"groups": other},
                            ).wait_recv()

    def over_step(step, act):
        @pl.loop(0, 4 if step else 2)
        def _(turn):
            half = lax.rem(turn, 2)
            block = z - step + 2 * step * lax.div(turn, 2)

            @pl.when((block >= 0) & (block < n))
            def _():
                act(block, half)

    def last_step(block, half):
        relay(block, half)
        finish(block, half)

    for step in range(1, n):
        for half in range(2):
            @pl.when(z >= step)
            def _():
                block = z - step
                arrived(block, h, half)

                @pl.when(z < n - 1)
                def _():
                    right(block, half).start()

                across(block, half).start()
                twinned(0, block, h, half).start()

            @pl.when(z + step < n)
            def _():
                block = z + step
                arrived(block, h, half)

                @pl.when(z > 0)
                def _():
                    left(block, half).start()

                across(block, half).start()
                twinned(0, block, h, half).start()

        if step == 1:
            over_step(0, relay)
        at_end = (z == 0) | (z == n - 1)
        if step == 1:
            @pl.when(at_end)
            def _():
                embedding_here()
                over_step(0, finish)

        if step == min(2, n - 1):
            @pl.when(jnp.logical_not(at_end))
            def _():
                embedding_here()
                over_step(0, finish)

        if step > 1:
            over_step(step - 1, relay)
            over_step(step - 1, finish)
    over_step(n - 1, last_step)

    @pl.when(z < n - 1)
    def _():
        for copy in halo_copies():
            copy.wait_send()

        @pl.loop(0, chunks)
        def _(c):
            state_copy(c).wait_send()

    for slot_of, target in ((0, twin), (1, side), (2, twin)):
        share_copy(slot_of, target).wait_send()
    for rank in range(n):
        @pl.when(z != rank)
        def _():
            for part in range(PARTS):
                w_copy(rank, part).wait_send()

        @pl.when(z == rank)
        def _():
            for source in range(n):
                for part in range(PARTS):
                    for hop in range(1, groups if source != rank else 1):
                        w_forward(rank, source, part, hop).wait_send()

    for block in range(n):
        for half in range(2):
            @pl.when((z < n - 1) & (z >= block))
            def _():
                right(block, half).wait_send()

            @pl.when((z > 0) & (z <= block))
            def _():
                left(block, half).wait_send()

            across(block, half).wait_send()
            twinned(0, block, h, half).wait_send()
            twinned(1, block, side, half).wait_send()

    parts[me] = marks[z, :, pl.ds(pl.multiple_of(h * TILE, TILE), TILE)]

    @pl.loop(1, total_peers)
    def _(k):
        there, where_head = peer(k)
        flat = there * heads + where_head
        remote(
            parts.at[flat], parts.at[flat], mark_send.at[there, where_head], mark_recv.at[flat],
            {"seq": there, "head": where_head},
        ).wait()

    peak = parts[0, 0:1, :]
    for flat in range(1, total_peers):
        peak = jnp.maximum(peak, parts[flat, 0:1, :])
    total = jnp.zeros((1, TILE), jnp.float32)
    picked = jnp.zeros((1, TILE), jnp.float32)
    for flat in range(total_peers):
        total = total + parts[flat, 1:2, :] * jnp.exp(parts[flat, 0:1, :] - peak)
        picked = picked + parts[flat, 2:3, :]
    losses = peak + jnp.log(total) - picked
    member_shape = sums.shape[1:]
    position = along(member_shape, 1) + h * TILE
    member = document(position) == lax.broadcasted_iota(jnp.int32, member_shape, 0) + 1
    mine = jnp.sum(jnp.where(member, losses, 0.0), axis=1, keepdims=True)
    sums[me] = jnp.broadcast_to(mine, sums.shape[1:])

    def sum_copy(k, slot_of):
        there, where_head = peer(k)
        return remote(
            sums.at[slot_of], sums.at[slot_of], sum_send.at[k], sum_recv.at[slot_of],
            {"seq": there, "head": where_head},
        )

    @pl.loop(1, total_peers)
    def _(k):
        sum_copy(k, me).start()

    @pl.loop(1, total_peers)
    def _(k):
        sum_copy(k, lax.rem(me + k, total_peers)).wait()

    grand = sums[0]
    for flat in range(1, total_peers):
        grand = grand + sums[flat]
    out_ref[...] = grand


def widths_of(columns, n):
    tiles = columns // TILE
    counts = [tiles // n + (rank < tiles % n) for rank in range(n)]
    if n > 2:
        counts[1] += 1
        counts[n - 1] -= 1
    return tuple(count * TILE for count in counts)


def fits(length, inner_here, share, depth, columns, n, heads, groups):
    widths = widths_of(columns, n)
    features = n * depth
    room = 2 * features * (n * length + max(widths) + inner_here)
    room += 4 * (length * inner_here * 4 + 6 * length * share + length * length)
    even = [inner_here % TILE, share % TILE, columns % TILE, depth % (groups * PARTS * 16)]
    even += [length % SPAN, length % (2 * LOSS_ROWS), length - heads * TILE, heads - 4]
    even += [share * heads - features]
    return not any(even) and n > 1 and min(widths) > 0 and room < 56 * 2**20


def block_stage(operands, scalars, whole, n, heads, groups):
    x_in, res = operands[0], operands[5]
    out_weight, lm_weight = whole
    length, inner_here = x_in.shape
    share = res.shape[1]
    features = out_weight.shape[1]
    widths = widths_of(lm_weight.shape[1], n)
    width = max(widths)
    peers = n * heads
    chunks = inner_here // TILE
    result = (-(-scalars[0].shape[0] // 8) * 8, TILE)
    dma = pltpu.SemaphoreType.DMA
    vmem = pltpu.VMEM
    f32, bf16 = jnp.float32, jnp.bfloat16
    return pl.pallas_call(
        functools.partial(block_kernel, n, heads, groups, inner_here * heads, features, widths),
        out_shape=[
            jax.ShapeDtypeStruct((length, share), bf16),
            jax.ShapeDtypeStruct(result, f32),
        ],
        in_specs=[pl.BlockSpec(memory_space=pltpu.VMEM)] * len(operands)
        + [pl.BlockSpec(memory_space=pltpu.SMEM)] * len(scalars)
        + [pl.BlockSpec(memory_space=pl.ANY)] * 2,
        out_specs=[pl.BlockSpec(memory_space=pltpu.VMEM)] * 2,
        scratch_shapes=[
            vmem((inner_here, features), bf16),
            vmem((features, width), bf16),
            vmem((n, length, features), bf16),
            vmem((n, heads, TILE), jnp.int32),
            vmem((n, 8, length), f32),
            vmem((peers, 8, TILE), f32),
            vmem((peers,) + result, f32),
            vmem((HALO, inner_here), bf16),
            vmem((HALO, 2 * STATE), bf16),
            vmem((length + HALO, TILE), f32),
            vmem((KERNEL - 1, length, TILE), f32),
            vmem((length, TILE), f32),
            vmem((chunks, 8, length), f32),
            vmem((chunks, length, 8), f32),
            vmem((length, inner_here), bf16),
            vmem((length, 2 * STATE), bf16),
            vmem((length, length), f32),
            vmem((chunks, TILE, STATE), f32),
            vmem((chunks, TILE, STATE), f32),
            vmem((length, inner_here), f32),
            vmem((length, TILE), f32),
            vmem((2, heads, 8, length), f32),
            vmem((length, inner_here), bf16),
            vmem((4, length, share), f32),
            vmem((3, length, share), f32),
            vmem((length, share), bf16),
            dma((2,)),
            dma((2,)),
            dma((2,)),
            dma((n, PARTS)),
            dma((n, PARTS)),
            dma((n, PARTS, groups)),
            dma((groups, n, PARTS)),
            dma((chunks,)),
            dma((chunks,)),
            dma((2, heads)),
            dma((2, heads)),
            dma((3,)),
            dma((3,)),
            dma((4, n, 2)),
            dma((n, 2)),
            dma((n, heads, 2)),
            dma((n,)),
            dma((n,)),
            dma((n, heads)),
            dma((peers,)),
            dma((peers,)),
            dma((peers,)),
        ],
        compiler_params=pltpu.CompilerParams(
            collective_id=0, has_side_effects=True, vmem_limit_bytes=63 * 2**20
        ),
        cost_estimate=pl.CostEstimate(
            flops=2 * n * length * features * width, bytes_accessed=4 * 10**7, transcendentals=10**7
        ),
    )(*operands, *scalars, *whole)


def fused_fits(residual, x_in, lm_weight):
    length, inner_here = x_in.shape
    depth, columns = lm_weight.shape
    sizes = [lax.axis_size(axis) for axis in ("seq", "head", "groups")]
    return fits(
        length, inner_here, residual.shape[1], depth, columns, *sizes
    )


def fused(
    residual,
    x_in,
    bc_in,
    z_in,
    dt_raw,
    dt_bias,
    decay_rate,
    d_skip,
    conv_x_weight,
    conv_x_bias,
    conv_bc_weight,
    conv_bc_bias,
    norm_gain,
    out_weight,
    final_gain,
    lm_weight,
    targets,
    doc_lengths,
):
    table = jnp.concatenate([conv_x_bias, norm_gain, conv_bc_bias, final_gain])
    operands = [
        x_in,
        z_in,
        bc_in,
        conv_x_weight,
        conv_bc_weight,
        residual,
        targets.reshape(-1, TILE),
        dt_raw,
        table.astype(jnp.float32).reshape(-1, TILE),
    ]
    scalars = [doc_lengths, dt_bias, decay_rate, d_skip]
    sizes = [lax.axis_size(axis) for axis in ("seq", "head", "groups")]
    block_out, sums = block_stage(operands, scalars, (out_weight, lm_weight), *sizes)
    sums = sums[: doc_lengths.shape[0], 0]
    return (block_out, sums / doc_lengths.astype(jnp.float32))


def local(
    residual,
    x_in,
    bc_in,
    z_in,
    dt_raw,
    dt_bias,
    decay_rate,
    d_skip,
    conv_x_weight,
    conv_x_bias,
    conv_bc_weight,
    conv_bc_bias,
    norm_gain,
    out_weight,
    final_gain,
    lm_weight,
    targets,
    doc_lengths,
):
    if fused_fits(residual, x_in, lm_weight):
        return fused(
            residual,
            x_in,
            bc_in,
            z_in,
            dt_raw,
            dt_bias,
            decay_rate,
            d_skip,
            conv_x_weight,
            conv_x_bias,
            conv_bc_weight,
            conv_bc_bias,
            norm_gain,
            out_weight,
            final_gain,
            lm_weight,
            targets,
            doc_lengths,
        )
    length = x_in.shape[0]
    inner_here = x_in.shape[1]
    heads_here = dt_raw.shape[0]
    seq_rank = lax.axis_index("seq")
    head_rank = lax.axis_index("head")
    offset_here = seq_rank * length
    positions = offset_here + jnp.arange(length, dtype=jnp.int32)
    doc_ids = document_of(positions, doc_lengths)
    columns_here = lm_weight.shape[1]
    devices = lax.axis_size("seq")
    width = -(-columns_here // (devices * 128)) * 128

    def window(rank):
        return jnp.minimum(rank * width, columns_here - width)

    depth = lm_weight.shape[0]
    vocab_weight = jnp.zeros((depth * devices, width), lm_weight.dtype)
    group = lax.axis_index("groups")
    groups = lax.axis_size("groups")
    band = depth // groups
    pieces = [
        lax.dynamic_slice(
            lm_weight, (group * band, window((seq_rank + by) % devices)), (band, width)
        )
        for by in range(1, devices)
    ]
    aims = [targets]
    for by in range(1, devices):
        aims.append(rotated(targets, "seq", by))
    margin = KERNEL - 1
    rims = shifted(
        jnp.concatenate([x_in[length - margin :], bc_in[length - margin :]], axis=1), "seq", 1
    )
    x_rim, bc_rim = rims[:, :inner_here], rims[:, inner_here:]
    keys_queries = causal_conv(
        bc_in, bc_rim, conv_bc_weight, conv_bc_bias, positions, doc_ids, doc_lengths
    )
    bmat, cmat = keys_queries[:, :STATE], keys_queries[:, STATE:]
    steps = jax.nn.softplus(dt_raw + dt_bias[:, None])
    climb = jnp.cumsum(steps * decay_rate[:, None], axis=1)
    before = document_of(jnp.reshape(offset_here - 1, (1,)), doc_lengths)[0]
    carried = (doc_ids == before).astype(jnp.float32)
    through = jnp.exp(-climb[:, length - 1]) * carried[length - 1]
    same = jnp.stack(
        [
            (document_of(positions - lag, doc_lengths) == doc_ids).astype(jnp.float32)
            for lag in range(KERNEL)
        ],
        axis=1,
    )
    last = (doc_ids == doc_ids[length - 1]).astype(jnp.float32)
    tail = jnp.exp(climb - climb[:, length - 1 :]) * last[None, :] * steps
    couples = heads_here // 2
    rows = jnp.concatenate(
        [climb.reshape(couples, 2, length), steps.reshape(couples, 2, length)], axis=1
    )
    cols = jnp.concatenate(
        [climb.reshape(couples, 2, length), tail.reshape(couples, 2, length)], axis=1
    ).transpose(0, 2, 1)
    rim = jnp.concatenate([jnp.zeros((8 - margin, inner_here), x_rim.dtype), x_rim], axis=0)
    values, own_end = conv_state(
        x_in,
        rim,
        conv_x_weight.astype(jnp.float32),
        conv_x_bias.astype(jnp.float32)[None, :],
        same,
        cols,
        bmat,
    )
    of_head = jnp.arange(inner_here, dtype=jnp.int32)[None, :] // HEAD_SIZE
    spread = (of_head == jnp.arange(heads_here, dtype=jnp.int32)[:, None]).astype(jnp.float32)
    incoming = entering(
        through, own_end.reshape(heads_here, HEAD_SIZE, STATE), "seq"
    ).reshape(inner_here, STATE)
    held_back = lax.optimization_barrier(tuple(pieces[1:]) + (incoming,))
    pieces, incoming = pieces[:1] + list(held_back[:-1]), held_back[-1]
    arrivals = []
    for by in range(1, devices):
        arrivals.append(rotated(pieces[by - 1], "seq", by))
    bands = []
    for by in range(1, devices):
        bands.append(
            [arrivals[by - 1]]
            + [rotated(arrivals[by - 1], "groups", hop) for hop in range(1, groups)]
        )
    order = jnp.arange(length, dtype=jnp.int32)
    inside = (doc_ids[:, None] == doc_ids[None, :]) & (order[:, None] >= order[None, :])
    scores = jnp.where(
        inside,
        lax.dot_general(
            cmat, bmat, (((1,), (1,)), ((), ())), preferred_element_type=jnp.float32
        ),
        0.0,
    )
    skip = jnp.dot(d_skip[None, :], spread, precision=HIGH)
    output = within(values, scores, cols, rows, skip)
    entry = jnp.dot((jnp.exp(-climb) * carried[None, :]).T, spread, precision=HIGH)
    arriving = lax.dot_general(
        cmat.astype(jnp.float32), incoming, (((1,), (1,)), ((), ())), precision=HALF
    )
    gated = (output + arriving * entry) * jax.nn.silu(z_in.astype(jnp.float32))
    square_sum = lax.psum(jnp.sum(gated * gated, axis=1), "head")
    scale = lax.rsqrt(square_sum / INNER + EPSILON)
    normed = (gated * scale[:, None] * norm_gain.astype(jnp.float32)[None, :]).astype(jnp.bfloat16)
    share = residual.shape[1]
    projected = scattered_product(normed, out_weight, "head")
    block_out = (residual.astype(jnp.float32) + projected).astype(jnp.bfloat16)
    widened = block_out.astype(jnp.float32)
    square_total = lax.psum(jnp.sum(widened * widened, axis=1), "head")
    gain_part = lax.dynamic_slice_in_dim(final_gain, head_rank * share, share, 0)
    final_scale = lax.rsqrt(square_total / D + EPSILON)
    hidden_part = (widened * final_scale[:, None] * gain_part.astype(jnp.float32)[None, :]).astype(
        jnp.bfloat16
    )
    own = lax.dynamic_slice_in_dim(lm_weight, window(seq_rank), width, 1)
    vocab_weight = lax.dynamic_update_slice_in_dim(vocab_weight, own, seq_rank * depth, 0)
    for by in range(1, devices):
        source = (seq_rank + devices - by) % devices
        for hop in range(groups):
            start = source * depth + (group + groups - hop) % groups * band
            vocab_weight = lax.dynamic_update_slice_in_dim(
                vocab_weight, bands[by - 1][hop], start, 0
            )
    column = jnp.arange(width, dtype=jnp.int32)
    first = head_rank * columns_here + window(seq_rank)
    live = column + window(seq_rank) >= seq_rank * width
    marks = jnp.zeros((3, length * devices), jnp.float32)
    for by in range(devices):
        source = (seq_rank + devices - by) % devices
        if by and by % 4 == 0:
            hidden_part, marks = lax.optimization_barrier((hidden_part, marks))
        rows = rotated(hidden_part, "seq", by) if by else hidden_part
        hidden = gathered_features(rows, "head")
        logits = jnp.dot(hidden, vocab_weight, preferred_element_type=jnp.float32)
        logits = jnp.where(live[None, :], logits, LOW)
        peak = jnp.max(logits, axis=1)
        wanted = aims[by] - first
        total = jnp.sum(jnp.exp(logits - peak[:, None]), axis=1)
        picked = jnp.sum(
            jnp.where((column[None, :] == wanted[:, None]) & live[None, :], logits, 0.0), axis=1
        )
        marks = lax.dynamic_update_slice_in_dim(
            marks, jnp.stack([peak, total, picked]), source * length, 1
        )
    for axis in ("head", "seq"):
        every_mark = lax.all_gather(marks, axis)
        peak = jnp.max(every_mark[:, 0], axis=0)
        total = jnp.sum(every_mark[:, 1] * jnp.exp(every_mark[:, 0] - peak[None]), axis=0)
        marks = jnp.stack([peak, total, jnp.sum(every_mark[:, 2], axis=0)])
    losses = marks[0] + jnp.log(marks[1]) - marks[2]
    every = document_of(jnp.arange(length * devices, dtype=jnp.int32), doc_lengths)
    documents = jnp.arange(doc_lengths.shape[0], dtype=jnp.int32)
    member = every[None, :] == documents[:, None]
    sums = jnp.sum(jnp.where(member, losses[None, :], 0.0), axis=1)
    return (block_out, sums / doc_lengths.astype(jnp.float32))


def solution(mesh):
    in_specs = (
        P(("groups", "seq"), "head"),
        P(("groups", "seq"), "head"),
        P(("groups", "seq"), None),
        P(("groups", "seq"), "head"),
        P("head", ("groups", "seq")),
        P("head"),
        P("head"),
        P("head"),
        P(None, "head"),
        P("head"),
        P(),
        P(),
        P("head"),
        P("head", None),
        P(),
        P("seq", "head"),
        P(("groups", "seq")),
        P("groups"),
    )
    out_specs = (P(("groups", "seq"), "head"), P("groups"))


    return jax.shard_map(local, mesh=mesh, in_specs=in_specs, out_specs=out_specs, check_vma=False)
```

profile of v0, /device:TPU:0, one launch (start us, length us, event | category | flops | bytes accessed | tf_op | source)
XLA Modules:
  0.0 184.6 jit_solution(3146868238103679892)
XLA Ops:
  0.6 1.4 fusion.table_ref
  2.0 0.0 copy-start
  2.0 179.3 %shard_map.185 = (bf16[512,640]{1,0:T(8,128)(2,1)}, f32[8,128]{1,0:T(8,128)}) custom-call(bf16[512,1280]{1,0:T(8,128)(2,1)} %x_ref.1, bf16[512,1280]{1,0:T(8,128)(2,1)} %z_ref.1, bf16[512,256]{1,0:T(8,128)(2,1)} %bc_ref.1, bf16[4,1280]{1,0:T(4,128)(2,1)} %taps_ref.1, bf16[4,256]{1,0:T(4,128)(2,1)} %bc_taps_ref.1, bf16[512,640]{1,0:T(8,128)(2,1)} %res_ref.1, ...), custom_call_target="tpu_custom_call" | custom-call | flops 18790481920 | bytes 40000000 | tf_op jit(solution)/shard_map/pallas_call | solution.py:940
  181.3 0.8 slice_reduce_fusion
  182.1 0.0 copy-done
  182.1 0.5 convert_divide_fusion
  182.6 2.0 %copy.21 = bf16[512,640]{1,0:T(8,128)(2,1)} copy(bf16[512,640]{1,0:T(8,128)(2,1)} %get-tuple-element.8) | data formatting | bytes 1310720
Async XLA Ops:
  2.0 180.1 %copy-start = (s32[4]{0:T(128)S(1)}, s32[4]{0:T(128)}, u32[]{:S(2)}) copy-start(s32[4]{0:T(128)} %lens_ref.1) | copy-start | bytes 52
where the time goes:
time: 185 us
  Pallas kernels  179 us (97%)
  local copies, waits for them, and re-layouts  2.76 us (1%)
  other arithmetic  1.87 us (1%)
    pallas_call x1, Pallas kernels, block_stage(): pl.pallas_call(functools.partial(block_kernel, n, heads, groups, inner_he...  179 us

commit v1 on v0

--- a/solution.py
+++ b/solution.py
@@ -220,6 +220,7 @@
 LOSS_ROWS = 256
 HALO = 16
 PARTS = 4
+SPLIT = 2
 
 
 def block_kernel(
@@ -335,14 +336,29 @@
         far_first = list(range(n - 1, rank, -1)) + list(range(rank))
         every = [(source, part) for source in far_first for part in range(PARTS)]
 
-        def early(source, part):
+        def stage(leg):
+            source, part = leg
+            if rank == 0:
+                return 0 if source == n - 1 and part < PARTS - 1 else 1 if source != 2 else 2
+            if source == rank - 1:
+                return 0 if part == 0 else 1 if rank in (1, n - 1) else 2
             if source < rank:
-                return source == rank - 1 and (part == 0 or rank in (1, n - 1))
-            if rank == 0:
-                return source != 2
-            return source > rank + 1 or (rank == n - 2 and part < PARTS // 2)
-
-        return [leg for leg in every if early(*leg)], [leg for leg in every if not early(*leg)]
+                return 1 if rank == n - 1 and part < PARTS - 1 and source == 0 else 2
+            return 1 if source > rank + 1 or (rank == n - 2 and part < PARTS // 2) else 2
+
+        staged = [[leg for leg in every if stage(leg) == which] for which in range(3)]
+        if rank > 0:
+            staged[1].sort(key=lambda leg: leg[1] if rank < n - 1 else -leg[0])
+        if rank < n - 1:
+            staged[2].sort(key=lambda leg: (-leg[0], leg[1]))
+        return staged
+
+    def pass_on_stage(which):
+        for rank in range(n):
+            @pl.when(z == rank)
+            def _():
+                for source, part in legs(rank)[which]:
+                    w_pass_on(rank, source, part)
 
     for rank in range(n):
         @pl.when(z > rank)
@@ -538,10 +554,13 @@
             for part in range(1, PARTS):
                 w_copy(rank, part).start()
 
+    for rank in range(n - 1, 1, -1):
         @pl.when(z + 1 < rank)
         def _():
             for part in range(PARTS):
                 w_copy(rank, part).start()
+
+    pass_on_stage(0)
 
     def tile_copy(which, k, slot_of):
         return remote(
@@ -597,11 +616,7 @@
     share_copy(2, twin).start()
     project(h, 3)
 
-    for rank in range(n):
-        @pl.when(z == rank)
-        def _():
-            for source, part in legs(rank)[0]:
-                w_pass_on(rank, source, part)
+    pass_on_stage(1)
 
     share_copy(2, twin).wait_recv()
     share_copy(1, side).wait_recv()
@@ -625,7 +640,8 @@
 
     full[z, :, pl.ds(pl.multiple_of(h * share, TILE), share)] = hid[...]
 
-    half_rows = length // 2
+    half_rows = length // SPLIT
+    logit_rows = min(LOSS_ROWS, half_rows)
 
     def near_of(half):
         start = half * half_rows
@@ -657,7 +673,7 @@
     def arrived(block, head, half):
         twinned(0, block, head, half).wait_recv()
 
-    for half in range(2):
+    for half in range(SPLIT):
         @pl.when(z < n - 1)
         def _():
             right(z, half, True).start()
@@ -683,18 +699,18 @@
     width = w_buf.shape[1]
 
     def compute(block, half):
-        @pl.loop(0, half_rows // LOSS_ROWS)
+        @pl.loop(0, half_rows // logit_rows)
         def _(step):
-            at = pl.multiple_of(half * half_rows + step * LOSS_ROWS, LOSS_ROWS)
+            at = pl.multiple_of(half * half_rows + step * logit_rows, logit_rows)
             logits = jnp.dot(
-                full[block, pl.ds(at, LOSS_ROWS), :], w_buf[...], preferred_element_type=jnp.float32
+                full[block, pl.ds(at, logit_rows), :], w_buf[...], preferred_element_type=jnp.float32
             )
             wanted = []
-            for cut in range(LOSS_ROWS // TILE):
+            for cut in range(logit_rows // TILE):
                 row = tgts[block, pl.ds(lax.div(at, TILE) + cut, 1), :]
                 wanted.append(jnp.transpose(jnp.broadcast_to(row, (TILE, TILE))))
             wanted = jnp.concatenate(wanted, axis=0) - start_column
-            lane = lax.broadcasted_iota(jnp.int32, (LOSS_ROWS, TILE), 1)
+            lane = lax.broadcasted_iota(jnp.int32, (logit_rows, TILE), 1)
             pieces = []
             for cut in range(0, width, TILE):
                 piece = logits[:, cut : cut + TILE]
@@ -705,8 +721,8 @@
             for piece in pieces[1:]:
                 peak = jnp.maximum(peak, piece)
             peak = jnp.max(peak, axis=1, keepdims=True)
-            total = jnp.zeros((LOSS_ROWS, TILE), jnp.float32)
-            picked = jnp.zeros((LOSS_ROWS, TILE), jnp.float32)
+            total = jnp.zeros((logit_rows, TILE), jnp.float32)
+            picked = jnp.zeros((logit_rows, TILE), jnp.float32)
             for index, piece in enumerate(pieces):
                 total = total + jnp.exp(piece - peak)
                 here = lane + index * TILE == wanted
@@ -716,9 +732,9 @@
             total = jnp.sum(total, axis=1, keepdims=True)
             picked = jnp.sum(picked, axis=1, keepdims=True)
             tile = jnp.where(lane == 0, peak, jnp.where(lane == 1, total, picked))
-            marks[block, :, pl.ds(at, LOSS_ROWS)] = jnp.transpose(tile)[0:8, :]
-
-        @pl.loop(half * (heads // 2), (half + 1) * (heads // 2))
+            marks[block, :, pl.ds(at, logit_rows)] = jnp.transpose(tile)[0:8, :]
+
+        @pl.loop(half * (heads // SPLIT), (half + 1) * (heads // SPLIT))
         def _(head):
             @pl.when((block != z) | (head != h))
             def _():
@@ -733,11 +749,7 @@
         arrived(block, lax.rem(twin + 2, heads), half)
         compute(block, half)
 
-    for rank in range(n):
-        @pl.when(z == rank)
-        def _():
-            for source, part in legs(rank)[1]:
-                w_pass_on(rank, source, part)
+    pass_on_stage(2)
 
     def embedding_here():
         for k in range(1, n):
@@ -758,11 +770,13 @@
                                 y_recv.at[other, source, part], {"groups": other},
                             ).wait_recv()
 
-    def over_step(step, act):
-        @pl.loop(0, 4 if step else 2)
+    def over_step(step, act, low=0, high=SPLIT):
+        span = high - low
+
+        @pl.loop(0, 2 * span if step else span)
         def _(turn):
-            half = lax.rem(turn, 2)
-            block = z - step + 2 * step * lax.div(turn, 2)
+            half = low + lax.rem(turn, span)
+            block = z - step + 2 * step * lax.div(turn, span)
 
             @pl.when((block >= 0) & (block < n))
             def _():
@@ -772,51 +786,78 @@
         relay(block, half)
         finish(block, half)
 
+    def from_left(step, half):
+        @pl.when(z >= step)
+        def _():
+            block = z - step
+            arrived(block, h, half)
+
+            @pl.when(z < n - 1)
+            def _():
+                right(block, half).start()
+
+            across(block, half).start()
+            twinned(0, block, h, half).start()
+
+    def from_right(step, half):
+        @pl.when(z + step < n)
+        def _():
+            block = z + step
+            arrived(block, h, half)
+
+            @pl.when(z > 0)
+            def _():
+                left(block, half).start()
+
+            across(block, half).start()
+            twinned(0, block, h, half).start()
+
+    @pl.when(z >= n // 2)
+    def _():
+        for half in range(SPLIT):
+            from_right(1, half)
+
+    at_end = (z == 0) | (z == n - 1)
     for step in range(1, n):
-        for half in range(2):
-            @pl.when(z >= step)
+        for half in range(SPLIT):
+            from_left(step, half)
+            if step > 1:
+                from_right(step, half)
+                continue
+
+            @pl.when(z < n // 2)
             def _():
-                block = z - step
-                arrived(block, h, half)
-
-                @pl.when(z < n - 1)
+                from_right(1, half)
+
+            if half == 0:
+                over_step(0, relay)
+
+                @pl.when(at_end)
                 def _():
-                    right(block, half).start()
-
-                across(block, half).start()
-                twinned(0, block, h, half).start()
-
-            @pl.when(z + step < n)
-            def _():
-                block = z + step
-                arrived(block, h, half)
-
-                @pl.when(z > 0)
-                def _():
-                    left(block, half).start()
-
-                across(block, half).start()
-                twinned(0, block, h, half).start()
-
-        if step == 1:
-            over_step(0, relay)
-        at_end = (z == 0) | (z == n - 1)
-        if step == 1:
+                    embedding_here()
+
             @pl.when(at_end)
             def _():
-                embedding_here()
-                over_step(0, finish)
-
-        if step == min(2, n - 1):
+                finish(z, half)
+
+        if step == 1:
             @pl.when(jnp.logical_not(at_end))
             def _():
                 embedding_here()
                 over_step(0, finish)
 
-        if step > 1:
+        elif step < n - 1:
             over_step(step - 1, relay)
             over_step(step - 1, finish)
-    over_step(n - 1, last_step)
+    if n > 2:
+        over_step(n - 2, relay)
+        over_step(n - 2, finish, 0, SPLIT - 1)
+        over_step(n - 1, relay, 0, 1)
+        over_step(n - 2, finish, SPLIT - 1, SPLIT)
+        over_step(n - 1, relay, 1, SPLIT)
+        over_step(n - 1, finish)
+    else:
+        over_step(n - 1, last_step)
 
     @pl.when(z < n - 1)
     def _():
@@ -843,7 +884,7 @@
                         w_forward(rank, source, part, hop).wait_send()
 
     for block in range(n):
-        for half in range(2):
+        for half in range(SPLIT):
             @pl.when((z < n - 1) & (z >= block))
             def _():
                 right(block, half).wait_send()
@@ -918,7 +959,7 @@
     room = 2 * features * (n * length + max(widths) + inner_here)
     room += 4 * (length * inner_here * 4 + 6 * length * share + length * length)
     even = [inner_here % TILE, share % TILE, columns % TILE, depth % (groups * PARTS * 16)]
-    even += [length % SPAN, length % (2 * LOSS_ROWS), length - heads * TILE, heads - 4]
+    even += [length % SPAN, length % LOSS_ROWS, length % (SPLIT * TILE), heads % SPLIT, length - heads * TILE, heads - 4]
     even += [share * heads - features]
     return not any(even) and n > 1 and min(widths) > 0 and room < 56 * 2**20
 
@@ -987,9 +1028,9 @@
             dma((2, heads)),
             dma((3,)),
             dma((3,)),
-            dma((4, n, 2)),
-            dma((n, 2)),
-            dma((n, heads, 2)),
+            dma((4, n, SPLIT)),
+            dma((n, SPLIT)),
+            dma((n, heads, SPLIT)),
             dma((n,)),
             dma((n,)),
             dma((n, heads)),

time: 185 us -> 181 us (0.978)
  Pallas kernels: 179 us -> 176 us
    pallas_call x1, Pallas kernels: 179 us -> 176 us  [block_stage(): pl.pallas_call(functools.partial(block_kernel, n, heads, groups, inner_he...]
where the time goes in v1:
time: 181 us
  Pallas kernels  176 us (97%)
  local copies, waits for them, and re-layouts  2.76 us (2%)
  other arithmetic  1.87 us (1%)
    pallas_call x1, Pallas kernels, block_stage(): pl.pallas_call(functools.partial(block_kernel, n, heads, groups, inner_he...  176 us

profile of v1, /device:TPU:0, one launch (start us, length us, event | category | flops | bytes accessed | tf_op | source)
XLA Modules:
  0.0 181.0 jit_solution(17570037903165573772)
XLA Ops:
  0.6 1.4 fusion.table_ref
  2.0 0.0 copy-start
  2.0 175.7 %shard_map.185 = (bf16[512,640]{1,0:T(8,128)(2,1)}, f32[8,128]{1,0:T(8,128)}) custom-call(bf16[512,1280]{1,0:T(8,128)(2,1)} %x_ref.1, bf16[512,1280]{1,0:T(8,128)(2,1)} %z_ref.1, bf16[512,256]{1,0:T(8,128)(2,1)} %bc_ref.1, bf16[4,1280]{1,0:T(4,128)(2,1)} %taps_ref.1, bf16[4,256]{1,0:T(4,128)(2,1)} %bc_taps_ref.1, bf16[512,640]{1,0:T(8,128)(2,1)} %res_ref.1, ...), custom_call_target="tpu_custom_call" | custom-call | flops 18790481920 | bytes 40000000 | tf_op jit(solution)/shard_map/pallas_call | solution.py:981
  177.7 0.8 slice_reduce_fusion
  178.5 0.0 copy-done
  178.5 0.5 convert_divide_fusion
  179.0 2.0 %copy.21 = bf16[512,640]{1,0:T(8,128)(2,1)} copy(bf16[512,640]{1,0:T(8,128)(2,1)} %get-tuple-element.8) | data formatting | bytes 1310720
Async XLA Ops:
  2.0 176.5 %copy-start = (s32[4]{0:T(128)S(1)}, s32[4]{0:T(128)}, u32[]{:S(2)}) copy-start(s32[4]{0:T(128)} %lens_ref.1) | copy-start | bytes 52
